TPU v7x, 32 devices: a whole 2x2x4 slice. The times are simulated.
32 devices in a mesh: dp: 4 (over x, core), tensor: 8 (over z, y).
Axes of the slice: x: 2, y: 2, z: 4, core: 2. Of those that a mesh axis runs over, the one named last changes fastest.
Arguments:
- attn_out: bfloat16 [96, 8192], P('dp', 'tensor'), parts along dimension 0, may hold values from -6 to 6
- w_out: bfloat16 [8192, 7168], P('tensor'), may hold values from -0.0625 to 0.0625
- residual: bfloat16 [96, 7168], P(('dp', 'tensor')), parts along dimension 0, may hold values from -6 to 6
- norm_gain: float32 [7168], replicated, may hold values from 0.1 to 1.9
Outputs:
- new_stream: bfloat16 [96, 7168], P(('dp', 'tensor')), parts along dimension 0
- quantized: bfloat16 [96, 7168], P(('dp', 'tensor')), parts along dimension 0
- block_scales: float32 [96, 56], P(('dp', 'tensor')), parts along dimension 0
There are 4 independent parts, one for each index of `dp`. A program takes and returns all parts, laid end to end along the dimension named above; an argument that names none is the same for every part. Nothing has to cross between parts.
All inputs are finite; a program needn't handle non-finite values. Where the computation divides by a largest or mean magnitude, that divisor is 1e-20 or more.
Results may differ from a plain program's by a relative error of at most 0.0014.
Values sent between devices are 32-bit elements; how exact they have to be, the bound alone decides.
No kernel may reach another device: no remote copies, remote signals or barrier semaphores. Data moves between devices by JAX's collectives and lax.ppermute only.
A program may use at most 64 MiB of HBM per device.

v0:
```python
import functools
import jax
import jax.numpy as jnp
from jax import lax
from jax.experimental import pallas as pl
from jax.experimental.pallas import tpu as pltpu
from jax.sharding import PartitionSpec as P

BLOCK = 128
AXIS = "tensor"
MIB = 1024 * 1024
LEAD = 2
NEAR = 4
STRIP = 4


def up(value, step):
    return -(-value // step) * step


def product_kernel(lots, rows, strips, attn_hbm, w_ref, *refs):
    count = len(lots)
    outs, (attn_ref, w_buf, sems, attn_sem) = refs[:count], refs[count:]
    tokens = attn_ref.shape[0]
    blocks = w_ref.shape[1] // BLOCK
    held = [len(lot) * rows for lot in lots]
    first = [sum(up(h, 8) for h in held[:k]) for k in range(count + 1)]
    fetch = pltpu.make_async_copy(attn_hbm, attn_ref, attn_sem)
    fetch.start()
    spans = [pl.ds(start * BLOCK, wide * BLOCK) for start, wide in strips]
    copies = [pltpu.make_async_copy(w_ref.at[:, span], w_buf.at[:, span], sems.at[s]) for s, span in enumerate(spans)]
    for copy in copies[:LEAD]:
        copy.start()
    me = lax.axis_index(AXIS)
    pos = lax.broadcasted_iota(jnp.int32, (first[-1], tokens), 0)
    col = lax.broadcasted_iota(jnp.int32, (first[-1], tokens), 1)
    want = jnp.full_like(pos, -1)
    for k, lot in enumerate(lots):
        for f, mask in enumerate(lot):
            start = first[k] + f * rows
            here = (pos >= start) & (pos < start + rows)
            want = jnp.where(here, (me ^ mask) * rows + pos - start, want)
    pick = jnp.where(col == want, 1.0, 0.0).astype(jnp.bfloat16)
    fetch.wait()
    for copy in copies[LEAD:]:
        copy.start()
    mine = jnp.dot(pick, attn_ref[...], preferred_element_type=jnp.float32).astype(jnp.bfloat16)
    for s, (start, wide) in enumerate(strips):
        copies[s].wait()
        acc = jnp.dot(mine, w_buf[:, spans[s]], preferred_element_type=jnp.float32)
        for c in range(wide):
            for k, out in enumerate(outs):
                out[pl.ds(start + c, held[k], stride=blocks), :] = acc[
                    first[k] : first[k] + held[k], c * BLOCK : (c + 1) * BLOCK
                ]


def cut(blocks):
    return [(start, min(STRIP, blocks - start)) for start in range(0, blocks, STRIP)]


def product(attn, w, lots, rows):
    tokens, depth = attn.shape
    width = w.shape[1]
    strips = cut(width // BLOCK)
    return pl.pallas_call(
        functools.partial(product_kernel, lots, rows, strips),
        out_shape=[
            jax.ShapeDtypeStruct((len(lot) * rows * width // BLOCK, BLOCK), jnp.float32) for lot in lots
        ],
        in_specs=[pl.BlockSpec(memory_space=pl.ANY)] * 2,
        out_specs=[pl.BlockSpec(memory_space=pltpu.VMEM)] * len(lots),
        scratch_shapes=[
            pltpu.VMEM((tokens, depth), jnp.bfloat16),
            pltpu.VMEM((depth, width), jnp.bfloat16),
            pltpu.SemaphoreType.DMA((len(strips),)),
            pltpu.SemaphoreType.DMA,
        ],
        compiler_params=pltpu.CompilerParams(vmem_limit_bytes=40 * MIB),
        cost_estimate=pl.CostEstimate(
            flops=2 * tokens * depth * width, bytes_accessed=2 * depth * width, transcendentals=0
        ),
        name="product",
    )(pltpu.with_memory_space_constraint(attn, pltpu.HBM), pltpu.with_memory_space_constraint(w, pltpu.HBM))


def fold_kernel(*refs):
    ins, (keep_ref, send_ref) = refs[:-2], refs[-2:]
    half = keep_ref.shape[0]
    for out, start in ((keep_ref, 0), (send_ref, half)):
        lines = pl.ds(start, half)
        value = ins[0][lines, :]
        for ref in ins[1:]:
            value = value + ref[lines, :]
        out[...] = value


def fold(parts):
    half = jax.ShapeDtypeStruct((parts[0].shape[0] // 2, BLOCK), jnp.float32)
    return pl.pallas_call(
        fold_kernel,
        out_shape=[half] * 2,
        in_specs=[pl.BlockSpec(memory_space=pltpu.VMEM)] * len(parts),
        out_specs=[pl.BlockSpec(memory_space=pltpu.VMEM)] * 2,
        compiler_params=pltpu.CompilerParams(vmem_limit_bytes=12 * MIB),
        name="fold",
    )(*parts)


def tail_kernel(rows, gain_ref, *refs):
    terms, (new_ref, quant_ref, scale_ref, hid, nrm) = refs[:-5], refs[-5:]
    blocks = gain_ref.shape[0]
    line = lax.broadcasted_iota(jnp.int32, (blocks, BLOCK), 0)
    lane = lax.broadcasted_iota(jnp.int32, (blocks, BLOCK), 1)
    for j in range(rows):
        at = pl.ds(j * blocks, blocks)
        hidden = terms[0][at, :]
        for term in terms[1:]:
            hidden = hidden + term[at, :]
        hid[at, :] = hidden
        square = jnp.sum(jnp.sum(hidden * hidden, axis=0, keepdims=True), axis=1, keepdims=True)
        normed = hidden * lax.rsqrt(square / (blocks * BLOCK) + 1e-06) * gain_ref[...]
        peak = jnp.max(jnp.abs(normed), axis=1, keepdims=True) + 1e-06
        nrm[at, :] = normed * 448.0 / peak
        spread = jnp.where(line == lane, peak / 448.0, 0.0)
        scale_ref[pl.ds(j, 1), :] = jnp.sum(spread, axis=0, keepdims=True)[:, :blocks]
    for c in range(blocks):
        lanes = pl.ds(c * BLOCK, BLOCK)
        new_ref[:, lanes] = hid[pl.ds(c, rows, stride=blocks), :].astype(jnp.bfloat16)
        quant_ref[:, lanes] = nrm[pl.ds(c, rows, stride=blocks), :].astype(jnp.bfloat16)


def tail(gain, terms, rows):
    blocks = gain.shape[0]
    width = blocks * BLOCK
    return pl.pallas_call(
        functools.partial(tail_kernel, rows),
        out_shape=(
            jax.ShapeDtypeStruct((rows, width), jnp.bfloat16),
            jax.ShapeDtypeStruct((rows, width), jnp.bfloat16),
            jax.ShapeDtypeStruct((rows, blocks), jnp.float32),
        ),
        in_specs=[pl.BlockSpec(memory_space=pltpu.VMEM)] * (1 + len(terms)),
        out_specs=[pl.BlockSpec(memory_space=pltpu.VMEM)] * 3,
        scratch_shapes=[pltpu.VMEM((rows * blocks, BLOCK), jnp.float32)] * 2,
        compiler_params=pltpu.CompilerParams(vmem_limit_bytes=8 * MIB),
        name="tail",
    )(gain, *terms)


def local(attn_out, w_out, residual, norm_gain):
    groups = lax.axis_size(AXIS)
    rows, width = residual.shape
    blocks = width // BLOCK
    if groups < 2 * NEAR or groups & (groups - 1):
        raise ValueError("groups")
    far = groups // NEAR

    def swap(value, mask):
        return lax.ppermute(value, AXIS, [(i, i ^ mask) for i in range(groups)])

    spread = [f * NEAR for f in range(far)]
    low, high = spread[: far // 2], spread[far // 2 :]
    top = groups // 2
    lots = [[q + f for f in spread] for q in range(NEAR - 1)]
    lots += [[NEAR - 1 + f for f in low], [NEAR - 1 + f for f in high]]
    own, one, two, three, cross = product(attn_out, w_out, lots, rows)
    one, two = swap(one, 1), swap(two, 2)
    cross, three = swap(cross, NEAR - 1 + top), swap(three, NEAR - 1)
    keep, send = fold([own, one, two])
    terms = [keep, three, cross, swap(send, top)]
    while top > NEAR:
        top //= 2
        keep, send = fold(terms)
        terms = [keep, swap(send, top)]
    res = residual.astype(jnp.float32).reshape(rows * blocks, BLOCK)
    return tail(norm_gain.reshape(blocks, BLOCK), [res, *terms], rows)


def solution(mesh):
    return jax.shard_map(
        local,
        mesh=mesh,
        in_specs=(P("dp", "tensor"), P("tensor", None), P(("dp", "tensor"), None), P()),
        out_specs=(P(("dp", "tensor"), None), P(("dp", "tensor"), None), P(("dp", "tensor"), None)),
        check_vma=False,
    )
```

profile of v0, /device:TPU:0, one launch (start us, length us, event | category | flops | bytes accessed | tf_op | source)
XLA Modules:
  0.0 24.3 jit_solution(12205637903759982749)
XLA Ops:
  0.6 0.0 copy-start.1
  0.6 0.0 copy-start
  0.7 6.3 %product.1 = (f32[336,128]{1,0:T(8,128)S(1)}, f32[336,128]{1,0:T(8,128)S(1)}, f32[336,128]{1,0:T(8,128)S(1)}, f32[168,128]{1,0:T(8,128)S(1)}, f32[168,128]{1,0:T(8,128)S(1)}) custom-call(bf16[24,1024]{1,0:T(8,128)(2,1)} %attn_hbm.1, bf16[1024,7168]{1,0:T(8,128)(2,1)} %w_ref.1), custom_call_target="tpu_custom_call" | custom-call | flops 352321536 | bytes 14680064 | tf_op jit(solution)/shard_map/product/pallas_call | solution.py:66
  7.0 3.1 %collective-permute-start = (f32[336,128]{1,0:T(8,128)S(1)}, f32[336,128]{1,0:T(8,128)S(1)}, u32[]{:S(2)}, u32[]{:S(2)}) collective-permute-start(f32[336,128]{1,0:T(8,128)S(1)} %get-tuple-element.11), channel_id=1, source_target_pairs={{0,1},{1,0},{2,3},{3,2},{4,5},{5,4},{6,7},{7,6},{8,9},{9,8},{10,11... | collective-permute-start | bytes 516104 | tf_op jit(solution)/shard_map/ppermute | solution.py:160
  10.0 1.6 %collective-permute-start.1 = (f32[336,128]{1,0:T(8,128)S(1)}, f32[336,128]{1,0:T(8,128)S(1)}, u32[]{:S(2)}, u32[]{:S(2)}) collective-permute-start(f32[336,128]{1,0:T(8,128)S(1)} %get-tuple-element.12), channel_id=1, source_target_pairs={{0,2},{1,3},{2,0},{3,1},{4,6},{5,7},{6,4},{7,5},{8,10},{9,11},{10,... | collective-permute-start | bytes 516104 | tf_op jit(solution)/shard_map/ppermute | solution.py:160
  11.6 0.0 collective-permute-start.2
  11.6 4.9 %collective-permute-start.3 = (f32[168,128]{1,0:T(8,128)S(1)}, f32[168,128]{1,0:T(8,128)S(1)}, u32[]{:S(2)}, u32[]{:S(2)}) collective-permute-start(f32[168,128]{1,0:T(8,128)S(1)} %get-tuple-element.15), channel_id=1, source_target_pairs={{0,7},{1,6},{2,5},{3,4},{4,3},{5,2},{6,1},{7,0},{8,15},{9,14},{10,... | collective-permute-start | bytes 258056 | tf_op jit(solution)/shard_map/ppermute | solution.py:160
  16.6 0.0 collective-permute-done.refs_1_
  16.6 0.2 collective-permute-done.1.refs_2_
  16.8 3.1 %collective-permute-start.4 = (f32[168,128]{1,0:T(8,128)S(1)}, f32[168,128]{1,0:T(8,128)S(1)}, u32[]{:S(2)}, u32[]{:S(2)}) collective-permute-start(f32[168,128]{1,0:T(8,128)S(1)} %get-tuple-element.16), channel_id=1, source_target_pairs={{0,4},{1,5},{2,6},{3,7},{4,0},{5,1},{6,2},{7,3},{8,12},{9,13},{10,... | collective-permute-start | bytes 258056 | tf_op jit(solution)/shard_map/ppermute | solution.py:160
  20.0 0.0 copy-done.1
  20.0 0.0 collective-permute-done.2.refs_2_
  20.0 2.5 %collective-permute-done.3.refs_3_ = f32[168,128]{1,0:T(8,128)S(1)} collective-permute-done((f32[168,128]{1,0:T(8,128)S(1)}, f32[168,128]{1,0:T(8,128)S(1)}, u32[]{:S(2)}, u32[]{:S(2)}) %collective-permute-start.3) | collective-permute-done | bytes 86048 | tf_op jit(solution)/shard_map/ppermute | solution.py:160
  22.5 0.9 %collective-permute-done.4.refs_4_ = f32[168,128]{1,0:T(8,128)S(1)} collective-permute-done((f32[168,128]{1,0:T(8,128)S(1)}, f32[168,128]{1,0:T(8,128)S(1)}, u32[]{:S(2)}, u32[]{:S(2)}) %collective-permute-start.4) | collective-permute-done | bytes 86048 | tf_op jit(solution)/shard_map/ppermute | solution.py:160
  23.4 0.0 copy-done
  23.4 0.9 %tail.1 = (bf16[3,7168]{1,0:T(4,128)(2,1)}, bf16[3,7168]{1,0:T(4,128)(2,1)}, f32[3,56]{1,0:T(4,128)}) custom-call(f32[56,128]{1,0:T(8,128)S(1)} %bitcast.1, f32[168,128]{1,0:T(8,128)S(1)} %reshape.18.refs_0_, f32[168,128]{1,0:T(8,128)S(1)} %get-tuple-element.13.refs_1_, f32[168,128]{1,0:T(8,128)S(1)} %collective-permute-done.2.refs_2_, ...), custom_call_target="tpu_custom_call" | custom-call | tf_op jit(solution)/shard_map/tail/pallas_call | solution.py:136
  (2 shorter events, 0.1 us)
Async XLA Ops:
  0.6 19.3 %copy-start.1 = (bf16[3,7168]{1,0:T(4,128)(2,1)S(1)}, bf16[3,7168]{1,0:T(4,128)(2,1)}, u32[]{:S(2)}) copy-start(bf16[3,7168]{1,0:T(4,128)(2,1)} %param.6) | copy-start | bytes 129028
  0.6 22.8 %copy-start = (f32[7168]{0:T(1024)S(1)}, f32[7168]{0:T(1024)}, u32[]{:S(2)}) copy-start(f32[7168]{0:T(1024)} %param.7) | copy-start | bytes 86020
  7.0 9.6 %collective-permute-start = (f32[336,128]{1,0:T(8,128)S(1)}, f32[336,128]{1,0:T(8,128)S(1)}, u32[]{:S(2)}, u32[]{:S(2)}) collective-permute-start(f32[336,128]{1,0:T(8,128)S(1)} %get-tuple-element.11), channel_id=1, source_target_pairs={{0,1},{1,0},{2,3},{3,2},{4,5},{5,4},{6,7},{7,6},{8,9},{9,8},{10,11... | collective-permute-start | bytes 516104 | tf_op jit(solution)/shard_map/ppermute | solution.py:160
  10.0 6.8 %collective-permute-start.1 = (f32[336,128]{1,0:T(8,128)S(1)}, f32[336,128]{1,0:T(8,128)S(1)}, u32[]{:S(2)}, u32[]{:S(2)}) collective-permute-start(f32[336,128]{1,0:T(8,128)S(1)} %get-tuple-element.12), channel_id=1, source_target_pairs={{0,2},{1,3},{2,0},{3,1},{4,6},{5,7},{6,4},{7,5},{8,10},{9,11},{10,... | collective-permute-start | bytes 516104 | tf_op jit(solution)/shard_map/ppermute | solution.py:160
  11.6 8.4 %collective-permute-start.2 = (f32[168,128]{1,0:T(8,128)S(1)}, f32[168,128]{1,0:T(8,128)S(1)}, u32[]{:S(2)}, u32[]{:S(2)}) collective-permute-start(f32[168,128]{1,0:T(8,128)S(1)} %get-tuple-element.14), channel_id=1, source_target_pairs={{0,3},{1,2},{2,1},{3,0},{4,7},{5,6},{6,5},{7,4},{8,11},{9,10},{10,... | collective-permute-start | bytes 258056 | tf_op jit(solution)/shard_map/ppermute | solution.py:160
  11.6 10.9 %collective-permute-start.3 = (f32[168,128]{1,0:T(8,128)S(1)}, f32[168,128]{1,0:T(8,128)S(1)}, u32[]{:S(2)}, u32[]{:S(2)}) collective-permute-start(f32[168,128]{1,0:T(8,128)S(1)} %get-tuple-element.15), channel_id=1, source_target_pairs={{0,7},{1,6},{2,5},{3,4},{4,3},{5,2},{6,1},{7,0},{8,15},{9,14},{10,... | collective-permute-start | bytes 258056 | tf_op jit(solution)/shard_map/ppermute | solution.py:160
  16.8 6.6 %collective-permute-start.4 = (f32[168,128]{1,0:T(8,128)S(1)}, f32[168,128]{1,0:T(8,128)S(1)}, u32[]{:S(2)}, u32[]{:S(2)}) collective-permute-start(f32[168,128]{1,0:T(8,128)S(1)} %get-tuple-element.16), channel_id=1, source_target_pairs={{0,4},{1,5},{2,6},{3,7},{4,0},{5,1},{6,2},{7,3},{8,12},{9,13},{10,... | collective-permute-start | bytes 258056 | tf_op jit(solution)/shard_map/ppermute | solution.py:160
where the time goes:
time: 24.5 us; the launch traced here: 24.3 us
  starting transfers between devices  12.7 us (52%)
  Pallas kernels  7.23 us (30%)
  waiting for transfers between devices  3.64 us (15%)
  between operations  0.67 us (3%)
    ppermute x5, starting transfers between devices, swap(): return lax.ppermute(value, AXIS, [(i, i ^ mask) for i in range(groups)])  12.7 us
    pallas_call x1, Pallas kernels, product(): pl.pallas_call(functools.partial(product_kernel, lots, rows, strips), out...  6.32 us
    ppermute x5, waiting for transfers between devices, swap(): return lax.ppermute(value, AXIS, [(i, i ^ mask) for i in range(groups)])  3.64 us
    pallas_call x1, Pallas kernels, tail(): pl.pallas_call(functools.partial(tail_kernel, rows), out_shape=(jax.Shape...  0.88 us
  transfers between devices with their start and end apart: 5, of which 3 were waited for; matrix products, arithmetic and copies ran while one was open for 0% of the time, Pallas kernels for 0%

commit v1 on v0

--- a/solution.py
+++ b/solution.py
@@ -85,23 +85,20 @@
 
 
 def fold_kernel(*refs):
-    ins, (keep_ref, send_ref) = refs[:-2], refs[-2:]
-    half = keep_ref.shape[0]
-    for out, start in ((keep_ref, 0), (send_ref, half)):
-        lines = pl.ds(start, half)
-        value = ins[0][lines, :]
-        for ref in ins[1:]:
-            value = value + ref[lines, :]
-        out[...] = value
+    ins, send_ref = refs[:-1], refs[-1]
+    half = send_ref.shape[0]
+    value = ins[0][pl.ds(half, half), :]
+    for ref in ins[1:]:
+        value = value + ref[pl.ds(half, half), :]
+    send_ref[...] = value
 
 
 def fold(parts):
-    half = jax.ShapeDtypeStruct((parts[0].shape[0] // 2, BLOCK), jnp.float32)
     return pl.pallas_call(
         fold_kernel,
-        out_shape=[half] * 2,
+        out_shape=jax.ShapeDtypeStruct((parts[0].shape[0] // 2, BLOCK), jnp.float32),
         in_specs=[pl.BlockSpec(memory_space=pltpu.VMEM)] * len(parts),
-        out_specs=[pl.BlockSpec(memory_space=pltpu.VMEM)] * 2,
+        out_specs=pl.BlockSpec(memory_space=pltpu.VMEM),
         compiler_params=pltpu.CompilerParams(vmem_limit_bytes=12 * MIB),
         name="fold",
     )(*parts)
@@ -167,12 +164,13 @@
     own, one, two, three, cross = product(attn_out, w_out, lots, rows)
     one, two = swap(one, 1), swap(two, 2)
     cross, three = swap(cross, NEAR - 1 + top), swap(three, NEAR - 1)
-    keep, send = fold([own, one, two])
-    terms = [keep, three, cross, swap(send, top)]
+    send = fold([own, one, two])
+    terms = [own, one, two, three, cross, swap(send, top)]
     while top > NEAR:
         top //= 2
-        keep, send = fold(terms)
-        terms = [keep, swap(send, top)]
+        sums = functools.reduce(jnp.add, [term[: terms[-1].shape[0]] for term in terms])
+        half = sums.shape[0] // 2
+        terms = [sums[:half], swap(sums[half:], top)]
     res = residual.astype(jnp.float32).reshape(rows * blocks, BLOCK)
     return tail(norm_gain.reshape(blocks, BLOCK), [res, *terms], rows)
 

time: 24.5 us -> 24.5 us (level)
  no operation moved by 1% of the time
where the time goes in v1:
time: 24.5 us; the launch traced here: 24.3 us
  starting transfers between devices  12.7 us (52%)
  Pallas kernels  7.23 us (30%)
  waiting for transfers between devices  3.65 us (15%)
  between operations  0.67 us (3%)
    ppermute x5, starting transfers between devices, swap(): return lax.ppermute(value, AXIS, [(i, i ^ mask) for i in range(groups)])  12.7 us
    pallas_call x1, Pallas kernels, product(): pl.pallas_call(functools.partial(product_kernel, lots, rows, strips), out...  6.32 us
    ppermute x5, waiting for transfers between devices, swap(): return lax.ppermute(value, AXIS, [(i, i ^ mask) for i in range(groups)])  3.65 us
    pallas_call x1, Pallas kernels, tail(): pl.pallas_call(functools.partial(tail_kernel, rows), out_shape=(jax.Shape...  0.89 us
  transfers between devices with their start and end apart: 5, of which 3 were waited for; matrix products, arithmetic and copies ran while one was open for 0% of the time, Pallas kernels for 0%

profile of v1, /device:TPU:0, one launch (start us, length us, event | category | flops | bytes accessed | tf_op | source)
XLA Modules:
  0.0 24.3 jit_solution(9917544690414756954)
XLA Ops:
  0.6 0.0 copy-start.1
  0.6 0.0 copy-start
  0.7 6.3 %product.1 = (f32[336,128]{1,0:T(8,128)S(1)}, f32[336,128]{1,0:T(8,128)S(1)}, f32[336,128]{1,0:T(8,128)S(1)}, f32[168,128]{1,0:T(8,128)S(1)}, f32[168,128]{1,0:T(8,128)S(1)}) custom-call(bf16[24,1024]{1,0:T(8,128)(2,1)} %attn_hbm.1, bf16[1024,7168]{1,0:T(8,128)(2,1)} %w_ref.1), custom_call_target="tpu_custom_call" | custom-call | flops 352321536 | bytes 14680064 | tf_op jit(solution)/shard_map/product/pallas_call | solution.py:66
  7.0 3.1 %collective-permute-start = (f32[336,128]{1,0:T(8,128)S(1)}, f32[336,128]{1,0:T(8,128)S(1)}, u32[]{:S(2)}, u32[]{:S(2)}) collective-permute-start(f32[336,128]{1,0:T(8,128)S(1)} %get-tuple-element.9), channel_id=1, source_target_pairs={{0,1},{1,0},{2,3},{3,2},{4,5},{5,4},{6,7},{7,6},{8,9},{9,8},{10,11... | collective-permute-start | bytes 516104 | tf_op jit(solution)/shard_map/ppermute | solution.py:157
  10.0 1.6 %collective-permute-start.1 = (f32[336,128]{1,0:T(8,128)S(1)}, f32[336,128]{1,0:T(8,128)S(1)}, u32[]{:S(2)}, u32[]{:S(2)}) collective-permute-start(f32[336,128]{1,0:T(8,128)S(1)} %get-tuple-element.10), channel_id=1, source_target_pairs={{0,2},{1,3},{2,0},{3,1},{4,6},{5,7},{6,4},{7,5},{8,10},{9,11},{10,... | collective-permute-start | bytes 516104 | tf_op jit(solution)/shard_map/ppermute | solution.py:157
  11.6 0.0 collective-permute-start.2
  11.6 4.9 %collective-permute-start.3 = (f32[168,128]{1,0:T(8,128)S(1)}, f32[168,128]{1,0:T(8,128)S(1)}, u32[]{:S(2)}, u32[]{:S(2)}) collective-permute-start(f32[168,128]{1,0:T(8,128)S(1)} %get-tuple-element.12), channel_id=1, source_target_pairs={{0,7},{1,6},{2,5},{3,4},{4,3},{5,2},{6,1},{7,0},{8,15},{9,14},{10,... | collective-permute-start | bytes 258056 | tf_op jit(solution)/shard_map/ppermute | solution.py:157
  16.6 0.0 collective-permute-done.refs_1_.refs_2_
  16.6 0.2 collective-permute-done.1.refs_2_.refs_3_
  16.8 3.1 %collective-permute-start.4 = (f32[168,128]{1,0:T(8,128)S(1)}, f32[168,128]{1,0:T(8,128)S(1)}, u32[]{:S(2)}, u32[]{:S(2)}) collective-permute-start(f32[168,128]{1,0:T(8,128)S(1)} %fold.1), channel_id=1, source_target_pairs={{0,4},{1,5},{2,6},{3,7},{4,0},{5,1},{6,2},{7,3},{8,12},{9,13},{10,... | collective-permute-start | bytes 258056 | tf_op jit(solution)/shard_map/ppermute | solution.py:157
  20.0 0.0 copy-done.1
  20.0 0.0 collective-permute-done.2.refs_4_
  20.0 2.5 %collective-permute-done.3.refs_5_ = f32[168,128]{1,0:T(8,128)S(1)} collective-permute-done((f32[168,128]{1,0:T(8,128)S(1)}, f32[168,128]{1,0:T(8,128)S(1)}, u32[]{:S(2)}, u32[]{:S(2)}) %collective-permute-start.3) | collective-permute-done | bytes 86048 | tf_op jit(solution)/shard_map/ppermute | solution.py:157
  22.5 0.9 %collective-permute-done.4.refs_6_ = f32[168,128]{1,0:T(8,128)S(1)} collective-permute-done((f32[168,128]{1,0:T(8,128)S(1)}, f32[168,128]{1,0:T(8,128)S(1)}, u32[]{:S(2)}, u32[]{:S(2)}) %collective-permute-start.4) | collective-permute-done | bytes 86048 | tf_op jit(solution)/shard_map/ppermute | solution.py:157
  23.4 0.0 copy-done
  23.4 0.9 %tail.1 = (bf16[3,7168]{1,0:T(4,128)(2,1)}, bf16[3,7168]{1,0:T(4,128)(2,1)}, f32[3,56]{1,0:T(4,128)}) custom-call(f32[56,128]{1,0:T(8,128)S(1)} %bitcast.1, f32[168,128]{1,0:T(8,128)S(1)} %reshape.18.refs_0_, f32[336,128]{1,0:T(8,128)S(1)} %get-tuple-element.8.refs_0_.refs_1_, f32[336,128]{1,0:T(8,128)S(1)} %collective-permute-done.refs_1_.refs_2_, ...), custom_call_target="tpu_custom_call" | custom-call | tf_op jit(solution)/shard_map/tail/pallas_call | solution.py:133
  (2 shorter events, 0.1 us)
Async XLA Ops:
  0.6 19.3 %copy-start.1 = (bf16[3,7168]{1,0:T(4,128)(2,1)S(1)}, bf16[3,7168]{1,0:T(4,128)(2,1)}, u32[]{:S(2)}) copy-start(bf16[3,7168]{1,0:T(4,128)(2,1)} %param.6) | copy-start | bytes 129028
  0.6 22.8 %copy-start = (f32[7168]{0:T(1024)S(1)}, f32[7168]{0:T(1024)}, u32[]{:S(2)}) copy-start(f32[7168]{0:T(1024)} %param.7) | copy-start | bytes 86020
  7.0 9.6 %collective-permute-start = (f32[336,128]{1,0:T(8,128)S(1)}, f32[336,128]{1,0:T(8,128)S(1)}, u32[]{:S(2)}, u32[]{:S(2)}) collective-permute-start(f32[336,128]{1,0:T(8,128)S(1)} %get-tuple-element.9), channel_id=1, source_target_pairs={{0,1},{1,0},{2,3},{3,2},{4,5},{5,4},{6,7},{7,6},{8,9},{9,8},{10,11... | collective-permute-start | bytes 516104 | tf_op jit(solution)/shard_map/ppermute | solution.py:157
  10.0 6.8 %collective-permute-start.1 = (f32[336,128]{1,0:T(8,128)S(1)}, f32[336,128]{1,0:T(8,128)S(1)}, u32[]{:S(2)}, u32[]{:S(2)}) collective-permute-start(f32[336,128]{1,0:T(8,128)S(1)} %get-tuple-element.10), channel_id=1, source_target_pairs={{0,2},{1,3},{2,0},{3,1},{4,6},{5,7},{6,4},{7,5},{8,10},{9,11},{10,... | collective-permute-start | bytes 516104 | tf_op jit(solution)/shard_map/ppermute | solution.py:157
  11.6 8.4 %collective-permute-start.2 = (f32[168,128]{1,0:T(8,128)S(1)}, f32[168,128]{1,0:T(8,128)S(1)}, u32[]{:S(2)}, u32[]{:S(2)}) collective-permute-start(f32[168,128]{1,0:T(8,128)S(1)} %get-tuple-element.11), channel_id=1, source_target_pairs={{0,3},{1,2},{2,1},{3,0},{4,7},{5,6},{6,5},{7,4},{8,11},{9,10},{10,... | collective-permute-start | bytes 258056 | tf_op jit(solution)/shard_map/ppermute | solution.py:157
  11.6 10.9 %collective-permute-start.3 = (f32[168,128]{1,0:T(8,128)S(1)}, f32[168,128]{1,0:T(8,128)S(1)}, u32[]{:S(2)}, u32[]{:S(2)}) collective-permute-start(f32[168,128]{1,0:T(8,128)S(1)} %get-tuple-element.12), channel_id=1, source_target_pairs={{0,7},{1,6},{2,5},{3,4},{4,3},{5,2},{6,1},{7,0},{8,15},{9,14},{10,... | collective-permute-start | bytes 258056 | tf_op jit(solution)/shard_map/ppermute | solution.py:157
  16.8 6.6 %collective-permute-start.4 = (f32[168,128]{1,0:T(8,128)S(1)}, f32[168,128]{1,0:T(8,128)S(1)}, u32[]{:S(2)}, u32[]{:S(2)}) collective-permute-start(f32[168,128]{1,0:T(8,128)S(1)} %fold.1), channel_id=1, source_target_pairs={{0,4},{1,5},{2,6},{3,7},{4,0},{5,1},{6,2},{7,3},{8,12},{9,13},{10,... | collective-permute-start | bytes 258056 | tf_op jit(solution)/shard_map/ppermute | solution.py:157
